TPU v7x, 128 devices: a whole 4x4x4 slice. The times are simulated.
128 devices in a mesh: dp: 32 (over y, x, core), tensor: 4 (over z).
Axes of the slice: x: 4, y: 4, z: 4, core: 2. Of those that a mesh axis runs over, the one named last changes fastest.
Arguments:
- activations: bfloat16 [32768, 28672], P('dp', 'tensor'), may hold values from -6 to 6
- out_grads: bfloat16 [32768, 8192], P('dp', 'tensor'), may hold values from -6 to 6
- proj_in: bfloat16 [28672, 64], P('tensor'), may hold values from -0.03125 to 0.03125
- proj_out: bfloat16 [8192, 64], P('tensor'), may hold values from -0.0625 to 0.0625
- validation: bfloat16 [512, 4096], P('tensor', 'dp'), may hold values from -0.09375 to 0.09375
- doc_lengths: int32 [32, 32], P('dp'), may hold values from 0 to 1024, as said below
- owner_rows: int32 [32, 32], P('dp'), may hold values from 0 to 1023, as said below
Outputs:
- scores: bfloat16 [1024, 512], P('dp', 'tensor')
Inputs may be any that keep to these rules, and one draw needn't show every extreme that they name: `doc_lengths`: in each row the first 1 to 32 entries are positive and sum to 1024, the rest are zero; some row has 32 documents and some row a single document. `owner_rows`: A permutation of 0 to 1024 - 1 over all entries; with owner = row // 32, the slots of one row go to 32 distinct owners, exactly 1 slot to each.
All inputs are finite; a program needn't handle non-finite values.
Results may differ from a plain program's by a relative error of at most 0.0098.
Values may be sent and summed in bfloat16 or wider, within the bound.
A program may use at most 64 MiB of HBM per device.

v0:
```python
import jax
import jax.numpy as jnp
from jax import lax
from jax.sharding import PartitionSpec as P


def sent_to_all(array, axis):
    count = lax.axis_size(axis)
    return lax.all_to_all(
        jnp.broadcast_to(array[None], (count, *array.shape)), axis, 0, 0, tiled=True
    )


def over_copies(array, axis):
    everything = sent_to_all(array, axis)
    return jnp.sum(everything.astype(jnp.float32), axis=0)


def rate(sketch, validation):
    summed = lax.dot_general(
        sketch,
        lax.all_gather(validation, "dp", axis=1, tiled=True),
        (((1,), (1,)), ((), ())),
        preferred_element_type=jnp.float32,
    )
    return summed.astype(jnp.bfloat16)


def deliver(payload, out_rows, is_live):
    maxdoc = payload.shape[0]
    devices = lax.axis_size("dp")
    per_owner = max(1, maxdoc // devices)
    owners = out_rows // maxdoc
    out_slot = out_rows % maxdoc
    indices = jnp.arange(maxdoc, dtype=jnp.int32)
    same_owner = owners[None, :] == owners[:, None]
    earlier = indices[None, :] < indices[:, None]
    within = jnp.sum((same_owner & earlier).astype(jnp.int32), axis=1)
    target_pos = owners * per_owner + within
    positions = jnp.arange(devices * per_owner, dtype=jnp.int32)
    select = target_pos[None, :] == positions[:, None]
    packed = jnp.dot(
        select.astype(jnp.bfloat16), payload, preferred_element_type=jnp.float32
    ).astype(jnp.bfloat16)
    labels = (
        jnp.sum(select.astype(jnp.int32) * jnp.where(is_live, out_slot + 1, 0)[None, :], axis=1) - 1
    )
    gathered, got_labels = (
        lax.all_to_all(packed, "dp", split_axis=0, concat_axis=0, tiled=True),
        lax.all_to_all(labels, "dp", split_axis=0, concat_axis=0, tiled=True),
    )
    choose = (got_labels[None, :] == indices[:, None]).astype(jnp.bfloat16)
    return jnp.dot(choose, gathered, preferred_element_type=jnp.float32).astype(jnp.bfloat16)


def make_sketch(left_cols, grad_proj, member, scaling):
    tokens = left_cols.shape[0]
    outer_prod = (left_cols[:, :, None] * grad_proj[:, None, :]).reshape(tokens, -1)
    summed = jnp.dot(
        member, outer_prod, precision=lax.Precision.HIGHEST, preferred_element_type=jnp.float32
    )
    return (summed * scaling[:, None]).astype(jnp.bfloat16)


def shards(activations, out_grads, proj_in, proj_out, validation, doc_lengths, owner_rows):
    act_part = jnp.dot(activations, proj_in, preferred_element_type=jnp.float32)
    grad_part = jnp.dot(out_grads, proj_out, preferred_element_type=jnp.float32)
    act_proj, grad_proj = (
        over_copies(act_part.astype(jnp.bfloat16), "tensor").astype(jnp.float32),
        over_copies(grad_part.astype(jnp.bfloat16), "tensor").astype(jnp.float32),
    )
    lengths = doc_lengths[0]
    out_rows = owner_rows[0]
    tokens = act_proj.shape[0]
    starts = jnp.cumsum(lengths) - lengths
    positions = jnp.arange(tokens, dtype=jnp.int32)
    member = (
        (positions[None, :] >= starts[:, None])
        & (positions[None, :] < starts[:, None] + lengths[:, None])
    ).astype(jnp.float32)
    scaling = 1.0 / jnp.sqrt(jnp.maximum(lengths, 1).astype(jnp.float32))
    sketch = make_sketch(act_proj, grad_proj, member, scaling)
    is_live = lengths > 0
    owned = deliver(sketch, out_rows, is_live)
    result = rate(owned, validation)
    return result


def solution(mesh):
    placed = (
        P("dp", "tensor"),
        P("dp", "tensor"),
        P("tensor", None),
        P("tensor", None),
        P("tensor", "dp"),
        P("dp", None),
        P("dp", None),
    )
    return jax.shard_map(
        shards, mesh=mesh, in_specs=placed, out_specs=P("dp", "tensor"), check_vma=False
    )
```

profile of v0, /device:TPU:1, one launch (start us, length us, event | category | flops | bytes accessed | tf_op | source)
XLA Modules:
  0.0 90.9 jit_solution(5479747645591731733)
XLA Ops:
  6.5 3.7 %convolution_convert_fusion.2 = bf16[1024,64]{0,1:T(8,128)(2,1)S(1)} fusion(bf16[1024,2048]{1,0:T(8,128)(2,1)} %param.8, bf16[2048,64]{0,1:T(8,128)(2,1)} %param.10), kind=kOutput, calls=%fused_computation.7 | convolution fusion | flops 268500992 | bytes 4587520 | tf_op jit(solution)/shard_map/dot_general | solution.py:67
  10.2 0.9 broadcast_in_dim.6
  11.1 5.8 %all-to-all-start.2 = ((bf16[4,1024,64]{1,2,0:T(8,128)(2,1)}), bf16[4,1024,64]{1,2,0:T(8,128)(2,1)S(1)}, u32[]{:S(2)}, u32[]{:S(2)}) async-start(bf16[4,1024,64]{1,2,0:T(8,128)(2,1)} %broadcast_in_dim.6), calls=%async_computation.2 | async-start | bytes 1048576 | tf_op jit(solution)/shard_map/all_to_all | solution.py:9
  17.0 0.7 all-gather.2.cloned.1.call-update
  17.7 0.7 and_select_fusion.1
  18.3 0.7 fusion.16
  19.0 0.2 convert_reduce_fusion.2
  19.2 9.7 %convolution_convert_fusion.3 = bf16[1024,64]{0,1:T(8,128)(2,1)S(1)} fusion(bf16[1024,7168]{1,0:T(8,128)(2,1)} %param.7, bf16[7168,64]{0,1:T(8,128)(2,1)S(1)} %copy-done), kind=kOutput, calls=%fused_computation.8 | convolution fusion | flops 939589632 | bytes 15728640 | tf_op jit(solution)/shard_map/dot_general | solution.py:66
  29.1 0.9 broadcast_in_dim.5
  30.0 4.2 %all-to-all-start.1 = ((bf16[4,1024,64]{1,2,0:T(8,128)(2,1)}), bf16[4,1024,64]{1,2,0:T(8,128)(2,1)S(1)}, u32[]{:S(2)}, u32[]{:S(2)}) async-start(bf16[4,1024,64]{1,2,0:T(8,128)(2,1)} %broadcast_in_dim.5), calls=%async_computation.1 | async-start | bytes 1048576 | tf_op jit(solution)/shard_map/all_to_all | solution.py:9
  34.5 0.7 copy.20
  35.2 6.7 %all-to-all-done.1 = bf16[4,1024,64]{1,2,0:T(8,128)(2,1)S(1)} async-done(((bf16[4,1024,64]{1,2,0:T(8,128)(2,1)}), bf16[4,1024,64]{1,2,0:T(8,128)(2,1)S(1)}, u32[]{:S(2)}, u32[]{:S(2)}) %all-to-all-start.1) | async-done | bytes 524320 | tf_op jit(solution)/shard_map/all_to_all | solution.py:9
  42.0 9.8 %all-to-all-start = ((s32[32,1,1]{2,1,0:T(1,128)}), s32[32,1,1]{2,1,0:T(1,128)S(1)}, u32[]{:S(2)}, u32[]{:S(2)}) async-start(s32[32,1,1]{2,1,0:T(1,128)} %copy.20), calls=%async_computation | async-start | bytes 32768 | tf_op jit(solution)/shard_map/all_to_all | solution.py:50
  51.8 2.2 %broadcast_multiply_fusion = f32[1024,64,64]{0,2,1:T(8,128)S(1)} fusion(f32[1024,64]{0,1:T(8,128)S(1)} %convert_reduce_fusion, f32[1024,64]{0,1:T(8,128)S(1)} %convert_reduce_fusion.1), kind=kLoop, calls=%fused_computation | loop fusion | flops 4194304 | bytes 17301504 | tf_op jit(solution)/shard_map/mul | solution.py:58
  54.0 8.5 %fusion = bf16[32,4096]{1,0:T(8,128)(2,1)S(1)} fusion(f32[1024,4096]{0,1:T(8,128)S(1)} %bitcast.41, f32[32]{0:T(128)S(1)} %fusion.19, s32[32]{0:T(128)S(1)} %reduce.1, s32[32]{0:T(128)S(1)} %bitcast_subtract_fusion), kind=kOutput, calls=%fused_computation.2 | convolution fusion | flops 1610973184 | bytes 17039744 | tf_op jit(solution)/shard_map/dot_general | solution.py:59
  62.5 0.2 fusion.1
  62.7 0.5 broadcast.112
  63.2 0.8 reduce.2
  64.0 0.9 reshape.94
  64.9 7.4 %all-to-all-start.3 = ((bf16[32,2,2048]{2,1,0:T(2,128)(2,1)}), bf16[32,2,2048]{2,1,0:T(2,128)(2,1)S(1)}, u32[]{:S(2)}, u32[]{:S(2)}) async-start(bf16[32,2,2048]{2,1,0:T(2,128)(2,1)} %reshape.94), calls=%async_computation.3 | async-start | bytes 524288 | tf_op jit(solution)/shard_map/all_to_all | solution.py:49
  72.3 0.7 reduce
  73.0 8.2 %all-to-all-done.3 = bf16[32,2,2048]{2,1,0:T(2,128)(2,1)S(1)} async-done(((bf16[32,2,2048]{2,1,0:T(2,128)(2,1)}), bf16[32,2,2048]{2,1,0:T(2,128)(2,1)S(1)}, u32[]{:S(2)}, u32[]{:S(2)}) %all-to-all-start.3) | async-done | bytes 262176 | tf_op jit(solution)/shard_map/all_to_all | solution.py:49
  81.2 0.3 reshape.95
  81.5 2.6 %fusion.3 = bf16[32,128]{1,0:T(8,128)(2,1)} fusion(bf16[128,4096]{1,0:T(8,128)(2,1)} %all-gather.2.cloned.1.call-done, bf16[32,1,4096]{2,1,0:T(2,128)(2,1)S(1)} %reshape.95, s32[32]{0:T(128)S(1)} %reduce), kind=kOutput, calls=%fused_computation.9 | convolution fusion | flops 42079232 | bytes 1319040 | tf_op jit(solution)/shard_map/dot_general | solution.py:20
  (18 shorter events, 0.6 us)
Async XLA Ops:
  6.5 12.7 %copy-start = (bf16[7168,64]{0,1:T(8,128)(2,1)S(1)}, bf16[7168,64]{0,1:T(8,128)(2,1)}, u32[]{:S(2)}) copy-start(bf16[7168,64]{0,1:T(8,128)(2,1)} %param.9) | copy-start | bytes 2752516
  6.5 22.5 %copy-start.1 = (s32[1,32]{1,0:T(1,128)S(1)}, s32[1,32]{1,0:T(1,128)}, u32[]{:S(2)}) copy-start(s32[1,32]{1,0:T(1,128)} %param.12) | copy-start | bytes 388
  11.1 18.0 %all-to-all-start.2 = ((bf16[4,1024,64]{1,2,0:T(8,128)(2,1)}), bf16[4,1024,64]{1,2,0:T(8,128)(2,1)S(1)}, u32[]{:S(2)}, u32[]{:S(2)}) async-start(bf16[4,1024,64]{1,2,0:T(8,128)(2,1)} %broadcast_in_dim.6), calls=%async_computation.2 | async-start | bytes 1048576 | tf_op jit(solution)/shard_map/all_to_all | solution.py:9
  16.9 64.5 %all-gather.2.cloned.1.call-start = ((), (), s32[]{:S(2)}) async-start(), calls=%async_computation.4 | async-start | bytes 1081344 | tf_op jit(solution)/shard_map/all_gather | solution.py:22
  30.0 12.0 %all-to-all-start.1 = ((bf16[4,1024,64]{1,2,0:T(8,128)(2,1)}), bf16[4,1024,64]{1,2,0:T(8,128)(2,1)S(1)}, u32[]{:S(2)}, u32[]{:S(2)}) async-start(bf16[4,1024,64]{1,2,0:T(8,128)(2,1)} %broadcast_in_dim.5), calls=%async_computation.1 | async-start | bytes 1048576 | tf_op jit(solution)/shard_map/all_to_all | solution.py:9
  42.0 23.0 %all-to-all-start = ((s32[32,1,1]{2,1,0:T(1,128)}), s32[32,1,1]{2,1,0:T(1,128)S(1)}, u32[]{:S(2)}, u32[]{:S(2)}) async-start(s32[32,1,1]{2,1,0:T(1,128)} %copy.20), calls=%async_computation | async-start | bytes 32768 | tf_op jit(solution)/shard_map/all_to_all | solution.py:50
  64.9 16.3 %all-to-all-start.3 = ((bf16[32,2,2048]{2,1,0:T(2,128)(2,1)}), bf16[32,2,2048]{2,1,0:T(2,128)(2,1)S(1)}, u32[]{:S(2)}, u32[]{:S(2)}) async-start(bf16[32,2,2048]{2,1,0:T(2,128)(2,1)} %reshape.94), calls=%async_computation.3 | async-start | bytes 524288 | tf_op jit(solution)/shard_map/all_to_all | solution.py:49
Sparse Core Ops, SparseCore 0:
  19.9 45.2 all-gather.1
where the time goes:
time: 91.3 us; the launch traced here: 90.9 us
  starting transfers between devices  27.2 us (30%)
  matrix products  24.7 us (27%)
  waiting for transfers between devices  15.7 us (17%)
  between operations  13.5 us (15%)
  other arithmetic  5.62 us (6%)
  local copies, waits for them, and re-layouts  4.23 us (5%)
    all_to_all x2, starting transfers between devices, sent_to_all(): lax.all_to_all(jnp.broadcast_to(array[None], (count, *array.shape)), axis...  10.1 us
    all_to_all x1, starting transfers between devices, deliver(): lax.all_to_all(labels, 'dp', split_axis=0, concat_axis=0, tiled=True)  9.76 us
    dot_general x1, matrix products, shards(): act_part = jnp.dot(activations, proj_in, preferred_element_type=jnp.float32)  9.72 us
    dot_general x1, matrix products, make_sketch(): jnp.dot(member, outer_prod, precision=lax.Precision.HIGHEST, preferred_el...  8.49 us
    all_to_all x1, waiting for transfers between devices, deliver(): lax.all_to_all(packed, 'dp', split_axis=0, concat_axis=0, tiled=True)  8.21 us
    all_to_all x1, starting transfers between devices, deliver(): lax.all_to_all(packed, 'dp', split_axis=0, concat_axis=0, tiled=True)  7.38 us
    all_to_all x2, waiting for transfers between devices, sent_to_all(): lax.all_to_all(jnp.broadcast_to(array[None], (count, *array.shape)), axis...  6.74 us
    dot_general x1, matrix products, shards(): grad_part = jnp.dot(out_grads, proj_out, preferred_element_type=jnp.float32)  3.68 us
  transfers between devices with their start and end apart: 5, of which 2 were waited for; matrix products, arithmetic and copies ran while one was open for 30% of the time, Pallas kernels for 0%

commit v1 on v0

v1 whole, which is shorter than its diff:
```python
import jax
import jax.numpy as jnp
from jax import lax
from jax.experimental import pallas as pl
from jax.experimental.pallas import tpu as pltpu
from jax.sharding import PartitionSpec as P

MESH = pl.DeviceIdType.MESH
F32 = jnp.float32
BF16 = jnp.bfloat16

CH = 128
NCH = 8
NRS = 6
LAG = 4
NT = 4
ND = 32
SUB = CH // NT
AHEAD = 3


def bytes_wait(ref, sem):
    pltpu.make_async_copy(ref, ref, sem).wait()


def kernel(
    act_hbm, grad_hbm, pin_hbm, pout_hbm, val_hbm, len_hbm, own_hbm, out_hbm,
    act_v, grad_v, pin_v, pout_v, len_v, own_v,
    part, rsbuf, dbuf, full, vbuf, params, lab_out, lab_in, sc_out, sc_in,
    at_ref, lhs_ref, s_ref, out_v,
    act_sem, grad_sem, misc_sem,
    v_send, v_recv, vf_send, vf_recv, rs_send, rs_recv, ag_send, ag_recv,
    lab_send, lab_recv, sc_send, sc_recv,
):
    r = lax.axis_index("dp")
    t = lax.axis_index("tensor")
    core = lax.rem(r, 2)
    chip = r // 2
    sibling = chip * 2 + (1 - core)

    def act_copy(c):
        rows = pl.ds(pl.multiple_of(c * CH, CH), CH)
        return pltpu.make_async_copy(act_hbm.at[rows], act_v.at[rows], act_sem.at[c])

    def grad_copy(c):
        rows = pl.ds(pl.multiple_of(c * CH, CH), CH)
        return pltpu.make_async_copy(grad_hbm.at[rows], grad_v.at[rows], grad_sem.at[c])

    pin_copy = pltpu.make_async_copy(pin_hbm, pin_v, misc_sem.at[0])
    pout_copy = pltpu.make_async_copy(pout_hbm, pout_v, misc_sem.at[1])
    val_copy = pltpu.make_async_copy(val_hbm, vbuf.at[r], misc_sem.at[2])
    len_copy = pltpu.make_async_copy(len_hbm, len_v, misc_sem.at[3])
    own_copy = pltpu.make_async_copy(own_hbm, own_v, misc_sem.at[4])

    len_copy.start()
    own_copy.start()
    pin_copy.start()
    act_copy(0).start()
    pout_copy.start()
    grad_copy(0).start()
    val_copy.start()
    for c in range(1, AHEAD):
        act_copy(c).start()
        grad_copy(c).start()

    barrier = pltpu.get_barrier_semaphore()

    def greet(i, carry):
        other = lax.rem(r + i, ND)
        pl.semaphore_signal(barrier, inc=1, device_id=(other, t), device_id_type=MESH)
        return carry

    lax.fori_loop(1, ND, greet, 0)
    for d in range(1, NT):
        pl.semaphore_signal(
            barrier, inc=1, device_id=(r, lax.rem(t + d, NT)), device_id_type=MESH
        )

    len_copy.wait()
    own_copy.wait()
    lens = len_v[...].astype(F32)
    rows_out = own_v[...]
    owner = rows_out // ND
    slot = (rows_out - owner * ND).astype(F32)
    row_id = lax.broadcasted_iota(jnp.int32, (ND, ND), 0)
    col_id = lax.broadcasted_iota(jnp.int32, (ND, ND), 1)
    chosen = jnp.broadcast_to(owner, (ND, ND)) == row_id
    zero = jnp.zeros((ND, ND), F32)
    doc_at = jnp.sum(jnp.where(chosen, col_id.astype(F32), zero), axis=1, keepdims=True)
    slot_at = jnp.sum(
        jnp.where(chosen, jnp.broadcast_to(slot, (ND, ND)), zero), axis=1, keepdims=True
    )
    lens_all = jnp.broadcast_to(lens, (ND, ND))
    len_at = jnp.sum(jnp.where(chosen, lens_all, zero), axis=1, keepdims=True)
    end_at = jnp.sum(
        jnp.where(col_id.astype(F32) <= doc_at, lens_all, zero), axis=1, keepdims=True
    )
    start_at = end_at - len_at
    params[0] = jnp.broadcast_to(start_at, (ND, 128))
    params[1] = jnp.broadcast_to(end_at, (ND, 128))
    params[2] = jnp.broadcast_to(1.0 / jnp.sqrt(jnp.maximum(len_at, 1.0)), (ND, 128))
    slots_wide = jnp.broadcast_to(slot_at, (ND, 128))
    for i in range(ND):
        lab_out[i] = slots_wide[i : i + 1, :]
    s_ref[...] = jnp.zeros_like(s_ref)

    def multiply(c):
        rows = pl.ds(pl.multiple_of(c * CH, CH), CH)
        act_copy(c).wait()
        left = jnp.dot(act_v[rows, :], pin_v[...], preferred_element_type=F32)
        grad_copy(c).wait()
        right = jnp.dot(grad_v[rows, :], pout_v[...], preferred_element_type=F32)
        part[c] = jnp.concatenate([left, right], axis=1).astype(BF16)

    def scatter_copy(c, d):
        peer = lax.rem(t + d, NT)
        return pltpu.make_async_remote_copy(
            src_ref=part.at[c, pl.ds(pl.multiple_of(peer * SUB, SUB), SUB)],
            dst_ref=rsbuf.at[c, d - 1],
            send_sem=rs_send.at[c],
            recv_sem=rs_recv.at[c],
            device_id=(r, peer),
            device_id_type=MESH,
        )

    def direct_copy(c, d):
        peer = lax.rem(t + d, NT)
        return pltpu.make_async_remote_copy(
            src_ref=part.at[c],
            dst_ref=dbuf.at[c - NRS, d - 1],
            send_sem=rs_send.at[c],
            recv_sem=rs_recv.at[c],
            device_id=(r, peer),
            device_id_type=MESH,
        )

    def gather_copy(c, d):
        peer = lax.rem(t + d, NT)
        mine = full.at[c, pl.ds(pl.multiple_of(t * SUB, SUB), SUB)]
        return pltpu.make_async_remote_copy(
            src_ref=mine,
            dst_ref=mine,
            send_sem=ag_send.at[c],
            recv_sem=ag_recv.at[c],
            device_id=(r, peer),
            device_id_type=MESH,
        )

    def reduce(c):
        bytes_wait(rsbuf.at[c], rs_recv.at[c])
        mine = pl.ds(pl.multiple_of(t * SUB, SUB), SUB)
        total = part[c, mine, :].astype(F32)
        for d in range(NT - 1):
            total = total + rsbuf[c, d].astype(F32)
        full[c, mine, :] = total.astype(BF16)
        for d in (2, 1, 3):
            gather_copy(c, d).start()

    pin_copy.wait()
    pout_copy.wait()
    multiply(0)
    pl.semaphore_wait(barrier, ND - 1 + NT - 1)
    for d in (2, 1, 3):
        scatter_copy(0, d).start()

    val_copy.wait()

    def val_to(peer, send, recv, block):
        return pltpu.make_async_remote_copy(
            src_ref=vbuf.at[block],
            dst_ref=vbuf.at[block],
            send_sem=send,
            recv_sem=recv,
            device_id=(peer, t),
            device_id_type=MESH,
        )

    def val_out(i, carry):
        peer = lax.rem(chip + i, ND // 2) * 2 + core
        val_to(peer, v_send, v_recv, r).start()
        return carry

    lax.fori_loop(1, ND // 2, val_out, 0)
    val_to(sibling, vf_send, vf_recv, r).start()

    def lab_copy(i):
        peer = lax.rem(r + i, ND)
        return pltpu.make_async_remote_copy(
            src_ref=lab_out.at[peer],
            dst_ref=lab_in.at[r],
            send_sem=lab_send,
            recv_sem=lab_recv,
            device_id=(peer, t),
            device_id_type=MESH,
        )

    def lab_go(i, carry):
        lab_copy(i).start()
        return carry

    lax.fori_loop(1, ND, lab_go, 0)
    lab_in[r] = lab_out[r]

    def step(c, carry):
        @pl.when(c + (AHEAD - 1) < NCH)
        def _():
            act_copy(c + (AHEAD - 1)).start()
            grad_copy(c + (AHEAD - 1)).start()

        multiply(c)

        @pl.when(c < NRS)
        def _():
            for d in (2, 1, 3):
                scatter_copy(c, d).start()

        @pl.when(c >= NRS)
        def _():
            for d in (2, 1, 3):
                direct_copy(c, d).start()

        @pl.when(c >= LAG)
        def _():
            reduce(c - LAG)

        return carry

    lax.fori_loop(1, NCH, step, 0)
    for c in range(NCH - LAG, NRS):
        reduce(c)

    bytes_wait(vbuf.at[pl.ds(0, ND // 2 - 1)], v_recv)

    def val_forward(i, carry):
        block = lax.rem(chip + i, ND // 2) * 2 + core
        val_to(sibling, vf_send, vf_recv, block).start()
        return carry

    lax.fori_loop(1, ND // 2, val_forward, 0)

    bytes_wait(lab_in.at[pl.ds(0, ND - 1)], lab_recv)
    slots_in = jnp.concatenate([lab_in[i] for i in range(ND)], axis=0)
    lane = lax.broadcasted_iota(jnp.int32, (ND, 128), 1).astype(F32)
    place = (slots_in == lane).astype(F32)

    lane_a = lax.broadcasted_iota(jnp.int32, (64, 128), 1)
    row_a = lax.broadcasted_iota(jnp.int32, (64, 128), 0)
    pick = jnp.where(row_a < 32, 2 * row_a, 2 * (row_a - 32) + 1)
    spread = (lane_a == pick).astype(BF16)
    low = lax.broadcasted_iota(jnp.int32, (CH, 128), 1) < 64

    def sketch(c, total):
        both = total.astype(BF16)
        turned = lax.dot_general(
            spread, both, (((1,), (1,)), ((), ())), preferred_element_type=F32
        )
        at_ref[:, 0:CH] = turned[0:32]
        at_ref[:, CH : 2 * CH] = turned[32:64]
        rolled = pltpu.roll(total, 64, 1)
        upper = jnp.where(low, rolled, 0.0).astype(BF16)
        lower = jnp.where(low, 0.0, total).astype(BF16)
        rhs = jnp.concatenate([upper, lower], axis=0)
        base = jnp.asarray(c * CH, F32)
        pos = lax.broadcasted_iota(jnp.int32, (ND, CH), 1).astype(F32) + base
        member = ((pos >= params[0]) & (pos < params[1])).astype(F32)
        member = jnp.concatenate([member, member], axis=1)
        for k in range(32):
            lhs_ref[k * ND : (k + 1) * ND, :] = (at_ref[k : k + 1, :] * member).astype(BF16)
        s_ref[...] += jnp.dot(lhs_ref[...], rhs, preferred_element_type=F32)

    def sketch_gathered(c, carry):
        bytes_wait(rsbuf.at[c], ag_recv.at[c])
        sketch(c, full[c].astype(F32))
        return carry

    lax.fori_loop(0, NRS, sketch_gathered, 0)

    def sketch_direct(c, carry):
        bytes_wait(dbuf.at[c - NRS], rs_recv.at[c])
        total = part[c].astype(F32)
        for d in range(NT - 1):
            total = total + dbuf[c - NRS, d].astype(F32)
        sketch(c, total)
        return carry

    lax.fori_loop(NRS, NCH, sketch_direct, 0)

    bytes_wait(vbuf.at[pl.ds(0, ND // 2)], vf_recv)
    local = jnp.zeros((ND, 128), F32)
    for k in range(0, 32, 2):
        left = jnp.concatenate(
            [s_ref[k * ND : (k + 1) * ND, :], s_ref[(k + 1) * ND : (k + 2) * ND, :]], axis=1
        ).astype(BF16)
        right = jnp.concatenate([vbuf[k], vbuf[k + 1]], axis=1)
        local = local + lax.dot_general(
            left, right, (((1,), (1,)), ((), ())), preferred_element_type=F32
        )
    local = local * params[2]
    for i in range(ND):
        sc_out[i] = local[i : i + 1, :]

    def score_copy(i):
        peer = lax.rem(r + i, ND)
        return pltpu.make_async_remote_copy(
            src_ref=sc_out.at[peer],
            dst_ref=sc_in.at[r],
            send_sem=sc_send,
            recv_sem=sc_recv,
            device_id=(peer, t),
            device_id_type=MESH,
        )

    def score_go(i, carry):
        score_copy(i).start()
        return carry

    lax.fori_loop(1, ND, score_go, 0)
    sc_in[r] = sc_out[r]

    for c in range(NRS):
        bytes_wait(rsbuf.at[c], rs_send.at[c])
        bytes_wait(rsbuf.at[c], ag_send.at[c])
    for c in range(NRS, NCH):
        bytes_wait(dbuf.at[c - NRS], rs_send.at[c])
    bytes_wait(vbuf.at[pl.ds(0, ND // 2 - 1)], v_send)
    bytes_wait(vbuf.at[pl.ds(0, ND // 2)], vf_send)
    bytes_wait(lab_out.at[pl.ds(0, ND - 1)], lab_send)

    bytes_wait(sc_in.at[pl.ds(0, ND - 1)], sc_recv)
    came = jnp.concatenate([sc_in[i] for i in range(ND)], axis=0)
    placed = lax.dot_general(
        place.astype(BF16),
        came.astype(BF16),
        (((0,), (0,)), ((), ())),
        preferred_element_type=F32,
    )
    out_v[...] = placed[0:ND].astype(BF16)
    out_copy = pltpu.make_async_copy(out_v, out_hbm, misc_sem.at[5])
    out_copy.start()
    bytes_wait(sc_out.at[pl.ds(0, ND - 1)], sc_send)
    out_copy.wait()


def shards(activations, out_grads, proj_in, proj_out, validation, doc_lengths, owner_rows):
    tokens, width_in = activations.shape
    width_out = out_grads.shape[1]
    dma = pltpu.SemaphoreType.DMA
    any_spec = pl.BlockSpec(memory_space=pl.ANY)
    return pl.pallas_call(
        kernel,
        out_shape=jax.ShapeDtypeStruct((ND, 128), BF16),
        in_specs=[any_spec] * 7,
        out_specs=any_spec,
        scratch_shapes=[
            pltpu.VMEM((tokens, width_in), BF16),
            pltpu.VMEM((tokens, width_out), BF16),
            pltpu.VMEM((width_in, 64), BF16),
            pltpu.VMEM((width_out, 64), BF16),
            pltpu.VMEM((1, ND), jnp.int32),
            pltpu.VMEM((1, ND), jnp.int32),
            pltpu.VMEM((NCH, CH, 128), BF16),
            pltpu.VMEM((NRS, NT - 1, SUB, 128), BF16),
            pltpu.VMEM((NCH - NRS, NT - 1, CH, 128), BF16),
            pltpu.VMEM((NRS, CH, 128), BF16),
            pltpu.VMEM((ND, 128, 128), BF16),
            pltpu.VMEM((3, ND, 128), F32),
            pltpu.VMEM((ND, 1, 128), F32),
            pltpu.VMEM((ND, 1, 128), F32),
            pltpu.VMEM((ND, 1, 128), F32),
            pltpu.VMEM((ND, 1, 128), F32),
            pltpu.VMEM((32, 2 * CH), F32),
            pltpu.VMEM((32 * ND, 2 * CH), BF16),
            pltpu.VMEM((32 * ND, 128), F32),
            pltpu.VMEM((ND, 128), BF16),
            dma((NCH,)),
            dma((NCH,)),
            dma((6,)),
            dma,
            dma,
            dma,
            dma,
            dma((NCH,)),
            dma((NCH,)),
            dma((NRS,)),
            dma((NRS,)),
            dma,
            dma,
            dma,
            dma,
        ],
        compiler_params=pltpu.CompilerParams(collective_id=0, has_side_effects=True),
        name="sketch_scores",
    )(activations, out_grads, proj_in, proj_out, validation, doc_lengths, owner_rows)


def solution(mesh):
    placed = (
        P("dp", "tensor"),
        P("dp", "tensor"),
        P("tensor", None),
        P("tensor", None),
        P("tensor", "dp"),
        P("dp", None),
        P("dp", None),
    )
    return jax.shard_map(
        shards, mesh=mesh, in_specs=placed, out_specs=P("dp", "tensor"), check_vma=False
    )
```

time: 91.3 us -> 37.2 us (0.41)
  Pallas kernels: 0 us -> 31.1 us
  starting transfers between devices: 27.2 us -> 0 us
  matrix products: 24.7 us -> 0 us
  waiting for transfers between devices: 15.7 us -> 0 us
  between operations: 13.5 us -> 0.01 us
  other arithmetic: 5.62 us -> 0 us
  local copies, waits for them, and re-layouts: 4.23 us -> 5.89 us
    pallas_call x0 -> x1, Pallas kernels: none -> 31.1 us  [shards(): pl.pallas_call(kernel, out_shape=jax.ShapeDtypeStruct((ND, 128), BF16), i...]
    all_to_all x4 -> x0, starting transfers between devices: 27.2 us -> none  [the longest x2 10.1 us: sent_to_all(): lax.all_to_all(jnp.broadcast_to(array[None], (count, *array.shape)), axis...]
    dot_general x5 -> x0, matrix products: 24.7 us -> none  [the longest x1 9.72 us: shards(): act_part = jnp.dot(activations, proj_in, preferred_element_type=jnp.float32)]
    all_to_all x4 -> x0, waiting for transfers between devices: 15 us -> none  [the longest x1 8.21 us: deliver(): lax.all_to_all(packed, 'dp', split_axis=0, concat_axis=0, tiled=True)]
    unnamed x6 -> x3, local copies, waits for them, and re-layouts: 1.17 us -> 5.89 us
    mul x2 -> x0, other arithmetic: 2.87 us -> none  [the longest x1 2.19 us: make_sketch(): left_cols[:, :, None] * grad_proj[:, None, :]]
    broadcast_in_dim x2 -> x0, local copies, waits for them, and re-layouts: 1.76 us -> none  [sent_to_all(): jnp.broadcast_to(array[None], (count, *array.shape))]
    all_to_all x2 -> x0, other arithmetic: 1.45 us -> none  [the longest x1 0.79 us: deliver(): lax.all_to_all(packed, 'dp', split_axis=0, concat_axis=0, tiled=True)]
  transfers between devices with their start and end apart: 5 -> 0, of which waited for: 2 -> 0; matrix products, arithmetic and copies ran while one was open for 30% -> 0% of each run, Pallas kernels for 0% -> 0%
where the time goes in v1:
time: 37.2 us; the launch traced here: 37 us
  Pallas kernels  31.1 us (84%)
  local copies, waits for them, and re-layouts  5.89 us (16%)
    pallas_call x1, Pallas kernels, shards(): pl.pallas_call(kernel, out_shape=jax.ShapeDtypeStruct((ND, 128), BF16), i...  31.1 us
    unnamed x3, local copies, waits for them, and re-layouts  5.89 us

profile of v1, /device:TPU:1, one launch (start us, length us, event | category | flops | bytes accessed | tf_op | source)
XLA Modules:
  0.0 37.0 jit_solution(2763569199196366482)
XLA Ops:
  0.0 2.0 %copy.9.pout_hbm = bf16[2048,64]{1,0:T(8,128)(2,1)} copy(bf16[2048,64]{0,1:T(8,128)(2,1)} %param.10) | data formatting | bytes 524288 | tf_op args[3]
  2.0 2.6 %copy.8.pin_hbm = bf16[7168,64]{1,0:T(8,128)(2,1)} copy(bf16[7168,64]{0,1:T(8,128)(2,1)} %param.9) | data formatting | bytes 1835008 | tf_op args[2]
  4.6 31.1 %sketch_scores.1 = bf16[32,128]{1,0:T(8,128)(2,1)} custom-call(bf16[1024,7168]{1,0:T(8,128)(2,1)} %act_hbm.1, bf16[1024,2048]{1,0:T(8,128)(2,1)} %grad_hbm.1, bf16[7168,64]{1,0:T(8,128)(2,1)} %copy.8.pin_hbm, bf16[2048,64]{1,0:T(8,128)(2,1)} %copy.9.pout_hbm, bf16[128,128]{1,0:T(8,128)(2,1)} %val_hbm.1, s32[1,32]{1,0:T(1,128)} %len_hbm.1, s32[1,32]{1,0:T(1,128)} %own_hbm.1), custom_call_target="tpu_custom_call" | custom-call | tf_op jit(solution)/shard_map/sketch_scores/pallas_call | solution.py:349
  35.7 1.3 %copy.11 = bf16[32,128]{1,0:T(8,128)(2,1)} copy(bf16[32,128]{1,0:T(8,128)(2,1)} %sketch_scores.1) | data formatting | bytes 16384

commit v2 on v1

--- a/solution.py
+++ b/solution.py
@@ -9,6 +9,7 @@
 F32 = jnp.float32
 BF16 = jnp.bfloat16
 
+NT_DIMS = (((1,), (1,)), ((), ()))
 CH = 128
 NCH = 8
 NRS = 6
@@ -107,9 +108,9 @@
     def multiply(c):
         rows = pl.ds(pl.multiple_of(c * CH, CH), CH)
         act_copy(c).wait()
-        left = jnp.dot(act_v[rows, :], pin_v[...], preferred_element_type=F32)
         grad_copy(c).wait()
-        right = jnp.dot(grad_v[rows, :], pout_v[...], preferred_element_type=F32)
+        left = lax.dot_general(act_v[rows, :], pin_v[...], NT_DIMS, preferred_element_type=F32)
+        right = lax.dot_general(grad_v[rows, :], pout_v[...], NT_DIMS, preferred_element_type=F32)
         part[c] = jnp.concatenate([left, right], axis=1).astype(BF16)
 
     def scatter_copy(c, d):
@@ -241,7 +242,11 @@
     bytes_wait(lab_in.at[pl.ds(0, ND - 1)], lab_recv)
     slots_in = jnp.concatenate([lab_in[i] for i in range(ND)], axis=0)
     lane = lax.broadcasted_iota(jnp.int32, (ND, 128), 1).astype(F32)
-    place = (slots_in == lane).astype(F32)
+    place = (slots_in == lane).astype(BF16)
+    eye = (row_id == col_id).astype(BF16)
+    place = lax.dot_general(
+        place, eye, (((0,), (0,)), ((), ())), preferred_element_type=F32
+    )[0:ND].astype(BF16)
 
     lane_a = lax.broadcasted_iota(jnp.int32, (64, 128), 1)
     row_a = lax.broadcasted_iota(jnp.int32, (64, 128), 0)
@@ -328,13 +333,8 @@
 
     bytes_wait(sc_in.at[pl.ds(0, ND - 1)], sc_recv)
     came = jnp.concatenate([sc_in[i] for i in range(ND)], axis=0)
-    placed = lax.dot_general(
-        place.astype(BF16),
-        came.astype(BF16),
-        (((0,), (0,)), ((), ())),
-        preferred_element_type=F32,
-    )
-    out_v[...] = placed[0:ND].astype(BF16)
+    placed = jnp.dot(place, came.astype(BF16), preferred_element_type=F32)
+    out_v[...] = placed.astype(BF16)
     out_copy = pltpu.make_async_copy(out_v, out_hbm, misc_sem.at[5])
     out_copy.start()
     bytes_wait(sc_out.at[pl.ds(0, ND - 1)], sc_send)
@@ -354,8 +354,8 @@
         scratch_shapes=[
             pltpu.VMEM((tokens, width_in), BF16),
             pltpu.VMEM((tokens, width_out), BF16),
-            pltpu.VMEM((width_in, 64), BF16),
-            pltpu.VMEM((width_out, 64), BF16),
+            pltpu.VMEM((64, width_in), BF16),
+            pltpu.VMEM((64, width_out), BF16),
             pltpu.VMEM((1, ND), jnp.int32),
             pltpu.VMEM((1, ND), jnp.int32),
             pltpu.VMEM((NCH, CH, 128), BF16),
@@ -390,7 +390,7 @@
         ],
         compiler_params=pltpu.CompilerParams(collective_id=0, has_side_effects=True),
         name="sketch_scores",
-    )(activations, out_grads, proj_in, proj_out, validation, doc_lengths, owner_rows)
+    )(activations, out_grads, proj_in.T, proj_out.T, validation, doc_lengths, owner_rows)
 
 
 def solution(mesh):

time: 37.2 us -> 31.3 us (0.84)
  local copies, waits for them, and re-layouts: 5.89 us -> 1.3 us
  Pallas kernels: 31.1 us -> 29.9 us
    unnamed x3 -> x1, local copies, waits for them, and re-layouts: 5.89 us -> 1.3 us
    pallas_call x1, Pallas kernels: 31.1 us -> 29.9 us  [shards(): pl.pallas_call(kernel, out_shape=jax.ShapeDtypeStruct((ND, 128), BF16), i...]
where the time goes in v2:
time: 31.3 us; the launch traced here: 31.2 us
  Pallas kernels  29.9 us (96%)
  local copies, waits for them, and re-layouts  1.3 us (4%)
    pallas_call x1, Pallas kernels, shards(): pl.pallas_call(kernel, out_shape=jax.ShapeDtypeStruct((ND, 128), BF16), i...  29.9 us
    unnamed x1, local copies, waits for them, and re-layouts  1.3 us

profile of v2, /device:TPU:1, one launch (start us, length us, event | category | flops | bytes accessed | tf_op | source)
XLA Modules:
  0.0 31.2 jit_solution(18230291616355254769)
XLA Ops:
  0.0 29.9 %sketch_scores.1 = bf16[32,128]{1,0:T(8,128)(2,1)} custom-call(bf16[1024,7168]{1,0:T(8,128)(2,1)} %act_hbm.1, bf16[1024,2048]{1,0:T(8,128)(2,1)} %grad_hbm.1, bf16[64,7168]{1,0:T(8,128)(2,1)} %bitcast.2, bf16[64,2048]{1,0:T(8,128)(2,1)} %bitcast.3, bf16[128,128]{1,0:T(8,128)(2,1)} %val_hbm.1, s32[1,32]{1,0:T(1,128)} %len_hbm.1, s32[1,32]{1,0:T(1,128)} %own_hbm.1), custom_call_target="tpu_custom_call" | custom-call | tf_op jit(solution)/shard_map/sketch_scores/pallas_call | solution.py:349
  29.9 1.3 %copy.9 = bf16[32,128]{1,0:T(8,128)(2,1)} copy(bf16[32,128]{1,0:T(8,128)(2,1)} %sketch_scores.1) | data formatting | bytes 16384

commit v3 on v2

--- a/solution.py
+++ b/solution.py
@@ -14,6 +14,10 @@
 NCH = 8
 NRS = 6
 LAG = 4
+SECOND = 5
+EARLY = 2
+MIDDLE = 2
+PAIR = 2 * CH
 NT = 4
 ND = 32
 SUB = CH // NT
@@ -30,13 +34,15 @@
     part, rsbuf, dbuf, full, vbuf, params, lab_out, lab_in, sc_out, sc_in,
     at_ref, lhs_ref, s_ref, out_v,
     act_sem, grad_sem, misc_sem,
-    v_send, v_recv, vf_send, vf_recv, rs_send, rs_recv, ag_send, ag_recv,
+    v_send, v_recv, rs_send, rs_recv, ag_send, ag_recv,
     lab_send, lab_recv, sc_send, sc_recv,
 ):
     r = lax.axis_index("dp")
     t = lax.axis_index("tensor")
     core = lax.rem(r, 2)
     chip = r // 2
+    x = lax.rem(chip, 4)
+    y = chip // 4
     sibling = chip * 2 + (1 - core)
 
     def act_copy(c):
@@ -49,7 +55,12 @@
 
     pin_copy = pltpu.make_async_copy(pin_hbm, pin_v, misc_sem.at[0])
     pout_copy = pltpu.make_async_copy(pout_hbm, pout_v, misc_sem.at[1])
-    val_copy = pltpu.make_async_copy(val_hbm, vbuf.at[r], misc_sem.at[2])
+    val_a_copy = pltpu.make_async_copy(
+        val_hbm.at[pl.ds(0, 64)], vbuf.at[core, 0, y, x], misc_sem.at[2]
+    )
+    val_b_copy = pltpu.make_async_copy(
+        val_hbm.at[pl.ds(64, 64)], vbuf.at[core, 1, x, y], misc_sem.at[6]
+    )
     len_copy = pltpu.make_async_copy(len_hbm, len_v, misc_sem.at[3])
     own_copy = pltpu.make_async_copy(own_hbm, own_v, misc_sem.at[4])
 
@@ -59,7 +70,8 @@
     act_copy(0).start()
     pout_copy.start()
     grad_copy(0).start()
-    val_copy.start()
+    val_a_copy.start()
+    val_b_copy.start()
     for c in range(1, AHEAD):
         act_copy(c).start()
         grad_copy(c).start()
@@ -157,32 +169,49 @@
         for d in (2, 1, 3):
             gather_copy(c, d).start()
 
+    def ahead(c):
+        @pl.when(c + (AHEAD - 1) < NCH)
+        def _():
+            act_copy(c + (AHEAD - 1)).start()
+            grad_copy(c + (AHEAD - 1)).start()
+
+    def early(c, carry):
+        @pl.when(c > 0)
+        def _():
+            ahead(c)
+
+        multiply(c)
+        return carry
+
     pin_copy.wait()
     pout_copy.wait()
-    multiply(0)
+    lax.fori_loop(0, EARLY, early, 0)
+    val_a_copy.wait()
+    val_b_copy.wait()
     pl.semaphore_wait(barrier, ND - 1 + NT - 1)
     for d in (2, 1, 3):
-        scatter_copy(0, d).start()
-
-    val_copy.wait()
-
-    def val_to(peer, send, recv, block):
-        return pltpu.make_async_remote_copy(
-            src_ref=vbuf.at[block],
-            dst_ref=vbuf.at[block],
+        for c in range(EARLY):
+            scatter_copy(c, d).start()
+
+    def val_to(peer, send, recv, ref):
+        return pltpu.make_async_remote_copy(
+            src_ref=ref,
+            dst_ref=ref,
             send_sem=send,
             recv_sem=recv,
             device_id=(peer, t),
             device_id_type=MESH,
         )
 
-    def val_out(i, carry):
-        peer = lax.rem(chip + i, ND // 2) * 2 + core
-        val_to(peer, v_send, v_recv, r).start()
-        return carry
-
-    lax.fori_loop(1, ND // 2, val_out, 0)
-    val_to(sibling, vf_send, vf_recv, r).start()
+    def along_x(d):
+        return (y * 4 + lax.rem(x + d, 4)) * 2 + core
+
+    def along_y(d):
+        return (lax.rem(y + d, 4) * 4 + x) * 2 + core
+
+    for d in (2, 1, 3):
+        val_to(along_x(d), v_send.at[0], v_recv.at[0], vbuf.at[core, 0, y, x]).start()
+        val_to(along_y(d), v_send.at[1], v_recv.at[1], vbuf.at[core, 1, x, y]).start()
 
     def lab_copy(i):
         peer = lax.rem(r + i, ND)
@@ -202,12 +231,15 @@
     lax.fori_loop(1, ND, lab_go, 0)
     lab_in[r] = lab_out[r]
 
+    def val_second():
+        bytes_wait(vbuf.at[0, 0, 0, pl.ds(0, 3)], v_recv.at[0])
+        bytes_wait(vbuf.at[0, 0, 0, pl.ds(0, 3)], v_recv.at[1])
+        for d in (2, 1, 3):
+            val_to(along_y(d), v_send.at[2], v_recv.at[2], vbuf.at[core, 0, y]).start()
+            val_to(along_x(d), v_send.at[3], v_recv.at[3], vbuf.at[core, 1, x]).start()
+
     def step(c, carry):
-        @pl.when(c + (AHEAD - 1) < NCH)
-        def _():
-            act_copy(c + (AHEAD - 1)).start()
-            grad_copy(c + (AHEAD - 1)).start()
-
+        ahead(c)
         multiply(c)
 
         @pl.when(c < NRS)
@@ -224,20 +256,15 @@
         def _():
             reduce(c - LAG)
 
-        return carry
-
-    lax.fori_loop(1, NCH, step, 0)
+        @pl.when(c == SECOND)
+        def _():
+            val_second()
+
+        return carry
+
+    lax.fori_loop(EARLY, NCH, step, 0)
     for c in range(NCH - LAG, NRS):
         reduce(c)
-
-    bytes_wait(vbuf.at[pl.ds(0, ND // 2 - 1)], v_recv)
-
-    def val_forward(i, carry):
-        block = lax.rem(chip + i, ND // 2) * 2 + core
-        val_to(sibling, vf_send, vf_recv, block).start()
-        return carry
-
-    lax.fori_loop(1, ND // 2, val_forward, 0)
 
     bytes_wait(lab_in.at[pl.ds(0, ND - 1)], lab_recv)
     slots_in = jnp.concatenate([lab_in[i] for i in range(ND)], axis=0)
@@ -252,51 +279,70 @@
     row_a = lax.broadcasted_iota(jnp.int32, (64, 128), 0)
     pick = jnp.where(row_a < 32, 2 * row_a, 2 * (row_a - 32) + 1)
     spread = (lane_a == pick).astype(BF16)
-    low = lax.broadcasted_iota(jnp.int32, (CH, 128), 1) < 64
-
-    def sketch(c, total):
-        both = total.astype(BF16)
+    low = lax.broadcasted_iota(jnp.int32, (PAIR, 128), 1) < 64
+
+    def sketch(p, total):
         turned = lax.dot_general(
-            spread, both, (((1,), (1,)), ((), ())), preferred_element_type=F32
-        )
-        at_ref[:, 0:CH] = turned[0:32]
-        at_ref[:, CH : 2 * CH] = turned[32:64]
+            spread, total.astype(BF16), NT_DIMS, preferred_element_type=F32
+        )
+        at_ref[:, 0:PAIR] = turned[0:32]
+        at_ref[:, PAIR : 2 * PAIR] = turned[32:64]
         rolled = pltpu.roll(total, 64, 1)
         upper = jnp.where(low, rolled, 0.0).astype(BF16)
         lower = jnp.where(low, 0.0, total).astype(BF16)
         rhs = jnp.concatenate([upper, lower], axis=0)
-        base = jnp.asarray(c * CH, F32)
-        pos = lax.broadcasted_iota(jnp.int32, (ND, CH), 1).astype(F32) + base
-        member = ((pos >= params[0]) & (pos < params[1])).astype(F32)
-        member = jnp.concatenate([member, member], axis=1)
+        pos = lax.broadcasted_iota(jnp.int32, (ND, 128), 1).astype(F32)
+        pieces = []
+        for i in range(PAIR // 128):
+            at = pos + jnp.asarray(p * PAIR + i * 128, F32)
+            pieces.append(((at >= params[0]) & (at < params[1])).astype(F32))
+        member = jnp.concatenate(pieces + pieces, axis=1)
         for k in range(32):
             lhs_ref[k * ND : (k + 1) * ND, :] = (at_ref[k : k + 1, :] * member).astype(BF16)
         s_ref[...] += jnp.dot(lhs_ref[...], rhs, preferred_element_type=F32)
 
-    def sketch_gathered(c, carry):
-        bytes_wait(rsbuf.at[c], ag_recv.at[c])
-        sketch(c, full[c].astype(F32))
-        return carry
-
-    lax.fori_loop(0, NRS, sketch_gathered, 0)
-
-    def sketch_direct(c, carry):
+    def sketch_gathered(p, carry):
+        for c in (2 * p, 2 * p + 1):
+            bytes_wait(rsbuf.at[c], ag_recv.at[c])
+        total = jnp.concatenate([full[2 * p], full[2 * p + 1]], axis=0)
+        sketch(p, total.astype(F32))
+        return carry
+
+    lax.fori_loop(0, MIDDLE, sketch_gathered, 0)
+
+    bytes_wait(vbuf.at[0, 0, pl.ds(0, 3)], v_recv.at[2])
+    bytes_wait(vbuf.at[0, 0, pl.ds(0, 3)], v_recv.at[3])
+    val_to(sibling, v_send.at[4], v_recv.at[4], vbuf.at[core]).start()
+
+    lax.fori_loop(MIDDLE, NRS // 2, sketch_gathered, 0)
+
+    def direct_total(c):
         bytes_wait(dbuf.at[c - NRS], rs_recv.at[c])
         total = part[c].astype(F32)
         for d in range(NT - 1):
             total = total + dbuf[c - NRS, d].astype(F32)
-        sketch(c, total)
-        return carry
-
-    lax.fori_loop(NRS, NCH, sketch_direct, 0)
-
-    bytes_wait(vbuf.at[pl.ds(0, ND // 2)], vf_recv)
+        return total
+
+    def sketch_direct(p, carry):
+        sketch(p, jnp.concatenate([direct_total(2 * p), direct_total(2 * p + 1)], axis=0))
+        return carry
+
+    lax.fori_loop(NRS // 2, NCH // 2, sketch_direct, 0)
+
+    bytes_wait(vbuf.at[0], v_recv.at[4])
     local = jnp.zeros((ND, 128), F32)
     for k in range(0, 32, 2):
         left = jnp.concatenate(
             [s_ref[k * ND : (k + 1) * ND, :], s_ref[(k + 1) * ND : (k + 2) * ND, :]], axis=1
         ).astype(BF16)
-        right = jnp.concatenate([vbuf[k], vbuf[k + 1]], axis=1)
+        ky, kx = k // 8, (k // 2) % 4
+        right = jnp.concatenate(
+            [
+                jnp.concatenate([vbuf[j, 0, ky, kx], vbuf[j, 1, kx, ky]], axis=0)
+                for j in range(2)
+            ],
+            axis=1,
+        )
         local = local + lax.dot_general(
             left, right, (((1,), (1,)), ((), ())), preferred_element_type=F32
         )
@@ -327,8 +373,10 @@
         bytes_wait(rsbuf.at[c], ag_send.at[c])
     for c in range(NRS, NCH):
         bytes_wait(dbuf.at[c - NRS], rs_send.at[c])
-    bytes_wait(vbuf.at[pl.ds(0, ND // 2 - 1)], v_send)
-    bytes_wait(vbuf.at[pl.ds(0, ND // 2)], vf_send)
+    for i in range(2):
+        bytes_wait(vbuf.at[0, 0, 0, pl.ds(0, 3)], v_send.at[i])
+        bytes_wait(vbuf.at[0, 0, pl.ds(0, 3)], v_send.at[2 + i])
+    bytes_wait(vbuf.at[0], v_send.at[4])
     bytes_wait(lab_out.at[pl.ds(0, ND - 1)], lab_send)
 
     bytes_wait(sc_in.at[pl.ds(0, ND - 1)], sc_recv)
@@ -362,23 +410,21 @@
             pltpu.VMEM((NRS, NT - 1, SUB, 128), BF16),
             pltpu.VMEM((NCH - NRS, NT - 1, CH, 128), BF16),
             pltpu.VMEM((NRS, CH, 128), BF16),
-            pltpu.VMEM((ND, 128, 128), BF16),
+            pltpu.VMEM((2, 2, 4, 4, 64, 128), BF16),
             pltpu.VMEM((3, ND, 128), F32),
             pltpu.VMEM((ND, 1, 128), F32),
             pltpu.VMEM((ND, 1, 128), F32),
             pltpu.VMEM((ND, 1, 128), F32),
             pltpu.VMEM((ND, 1, 128), F32),
-            pltpu.VMEM((32, 2 * CH), F32),
-            pltpu.VMEM((32 * ND, 2 * CH), BF16),
+            pltpu.VMEM((32, 2 * PAIR), F32),
+            pltpu.VMEM((32 * ND, 2 * PAIR), BF16),
             pltpu.VMEM((32 * ND, 128), F32),
             pltpu.VMEM((ND, 128), BF16),
             dma((NCH,)),
             dma((NCH,)),
-            dma((6,)),
-            dma,
-            dma,
-            dma,
-            dma,
+            dma((7,)),
+            dma((5,)),
+            dma((5,)),
             dma((NCH,)),
             dma((NCH,)),
             dma((NRS,)),

time: 31.3 us -> 31 us (level)
  Pallas kernels: 29.9 us -> 29.5 us
    pallas_call x1, Pallas kernels: 29.9 us -> 29.5 us  [shards(): pl.pallas_call(kernel, out_shape=jax.ShapeDtypeStruct((ND, 128), BF16), i...]
where the time goes in v3:
time: 31 us; the launch traced here: 30.8 us
  Pallas kernels  29.5 us (95%)
  local copies, waits for them, and re-layouts  1.3 us (4%)
    pallas_call x1, Pallas kernels, shards(): pl.pallas_call(kernel, out_shape=jax.ShapeDtypeStruct((ND, 128), BF16), i...  29.5 us
    unnamed x1, local copies, waits for them, and re-layouts  1.3 us

profile of v3, /device:TPU:1, one launch (start us, length us, event | category | flops | bytes accessed | tf_op | source)
XLA Modules:
  0.0 30.8 jit_solution(7963033057657285540)
XLA Ops:
  0.0 29.5 %sketch_scores.1 = bf16[32,128]{1,0:T(8,128)(2,1)} custom-call(bf16[1024,7168]{1,0:T(8,128)(2,1)} %act_hbm.1, bf16[1024,2048]{1,0:T(8,128)(2,1)} %grad_hbm.1, bf16[64,7168]{1,0:T(8,128)(2,1)} %bitcast.2, bf16[64,2048]{1,0:T(8,128)(2,1)} %bitcast.3, bf16[128,128]{1,0:T(8,128)(2,1)} %val_hbm.1, s32[1,32]{1,0:T(1,128)} %len_hbm.1, s32[1,32]{1,0:T(1,128)} %own_hbm.1), custom_call_target="tpu_custom_call" | custom-call | tf_op jit(solution)/shard_map/sketch_scores/pallas_call | solution.py:397
  29.5 1.3 %copy.9 = bf16[32,128]{1,0:T(8,128)(2,1)} copy(bf16[32,128]{1,0:T(8,128)(2,1)} %sketch_scores.1) | data formatting | bytes 16384

commit v4 on v3

--- a/solution.py
+++ b/solution.py
@@ -11,13 +11,14 @@
 
 NT_DIMS = (((1,), (1,)), ((), ()))
 CH = 128
-NCH = 8
-NRS = 6
+NCH = 1024 // CH
+NRS = 7
 LAG = 4
-SECOND = 5
+SECOND = 4
 EARLY = 2
 MIDDLE = 2
-PAIR = 2 * CH
+TOKENS_ROW = 1024
+PAIR = 256
 NT = 4
 ND = 32
 SUB = CH // NT
@@ -29,10 +30,10 @@
 
 
 def kernel(
-    act_hbm, grad_hbm, pin_hbm, pout_hbm, val_hbm, len_hbm, own_hbm, out_hbm,
+    act_hbm, grad_hbm, pin_hbm, pout_hbm, val_hbm, len_hbm, own_hbm, got_hbm, place_hbm,
     act_v, grad_v, pin_v, pout_v, len_v, own_v,
-    part, rsbuf, dbuf, full, vbuf, params, lab_out, lab_in, sc_out, sc_in,
-    at_ref, lhs_ref, s_ref, out_v,
+    part, rsbuf, dbuf, full, vbuf, params, lab_out, lab_in, sc_out,
+    at_ref, lhs_ref, s_ref, place_v,
     act_sem, grad_sem, misc_sem,
     v_send, v_recv, rs_send, rs_recv, ag_send, ag_recv,
     lab_send, lab_recv, sc_send, sc_recv,
@@ -274,6 +275,7 @@
     place = lax.dot_general(
         place, eye, (((0,), (0,)), ((), ())), preferred_element_type=F32
     )[0:ND].astype(BF16)
+    place_v[...] = place
 
     lane_a = lax.broadcasted_iota(jnp.int32, (64, 128), 1)
     row_a = lax.broadcasted_iota(jnp.int32, (64, 128), 0)
@@ -301,35 +303,27 @@
             lhs_ref[k * ND : (k + 1) * ND, :] = (at_ref[k : k + 1, :] * member).astype(BF16)
         s_ref[...] += jnp.dot(lhs_ref[...], rhs, preferred_element_type=F32)
 
-    def sketch_gathered(p, carry):
-        for c in (2 * p, 2 * p + 1):
+    def summed(c):
+        if c < NRS:
             bytes_wait(rsbuf.at[c], ag_recv.at[c])
-        total = jnp.concatenate([full[2 * p], full[2 * p + 1]], axis=0)
-        sketch(p, total.astype(F32))
-        return carry
-
-    lax.fori_loop(0, MIDDLE, sketch_gathered, 0)
-
-    bytes_wait(vbuf.at[0, 0, pl.ds(0, 3)], v_recv.at[2])
-    bytes_wait(vbuf.at[0, 0, pl.ds(0, 3)], v_recv.at[3])
-    val_to(sibling, v_send.at[4], v_recv.at[4], vbuf.at[core]).start()
-
-    lax.fori_loop(MIDDLE, NRS // 2, sketch_gathered, 0)
-
-    def direct_total(c):
+            return full[c].astype(F32)
         bytes_wait(dbuf.at[c - NRS], rs_recv.at[c])
         total = part[c].astype(F32)
         for d in range(NT - 1):
             total = total + dbuf[c - NRS, d].astype(F32)
         return total
 
-    def sketch_direct(p, carry):
-        sketch(p, jnp.concatenate([direct_total(2 * p), direct_total(2 * p + 1)], axis=0))
-        return carry
-
-    lax.fori_loop(NRS // 2, NCH // 2, sketch_direct, 0)
+    for p in range(TOKENS_ROW // PAIR):
+        if p == MIDDLE:
+            bytes_wait(vbuf.at[0, 0, pl.ds(0, 3)], v_recv.at[2])
+            bytes_wait(vbuf.at[0, 0, pl.ds(0, 3)], v_recv.at[3])
+            val_to(sibling, v_send.at[4], v_recv.at[4], vbuf.at[core]).start()
+        each = PAIR // CH
+        sketch(p, jnp.concatenate([summed(p * each + i) for i in range(each)], axis=0))
 
     bytes_wait(vbuf.at[0], v_recv.at[4])
+    place_copy = pltpu.make_async_copy(place_v, place_hbm, misc_sem.at[7])
+    place_copy.start()
     local = jnp.zeros((ND, 128), F32)
     for k in range(0, 32, 2):
         left = jnp.concatenate(
@@ -346,7 +340,7 @@
         local = local + lax.dot_general(
             left, right, (((1,), (1,)), ((), ())), preferred_element_type=F32
         )
-    local = local * params[2]
+    local = (local * params[2]).astype(BF16)
     for i in range(ND):
         sc_out[i] = local[i : i + 1, :]
 
@@ -354,7 +348,7 @@
         peer = lax.rem(r + i, ND)
         return pltpu.make_async_remote_copy(
             src_ref=sc_out.at[peer],
-            dst_ref=sc_in.at[r],
+            dst_ref=got_hbm.at[r],
             send_sem=sc_send,
             recv_sem=sc_recv,
             device_id=(peer, t),
@@ -366,7 +360,8 @@
         return carry
 
     lax.fori_loop(1, ND, score_go, 0)
-    sc_in[r] = sc_out[r]
+    own_score = pltpu.make_async_copy(sc_out.at[r], got_hbm.at[r], misc_sem.at[5])
+    own_score.start()
 
     for c in range(NRS):
         bytes_wait(rsbuf.at[c], rs_send.at[c])
@@ -379,14 +374,10 @@
     bytes_wait(vbuf.at[0], v_send.at[4])
     bytes_wait(lab_out.at[pl.ds(0, ND - 1)], lab_send)
 
-    bytes_wait(sc_in.at[pl.ds(0, ND - 1)], sc_recv)
-    came = jnp.concatenate([sc_in[i] for i in range(ND)], axis=0)
-    placed = jnp.dot(place, came.astype(BF16), preferred_element_type=F32)
-    out_v[...] = placed.astype(BF16)
-    out_copy = pltpu.make_async_copy(out_v, out_hbm, misc_sem.at[5])
-    out_copy.start()
     bytes_wait(sc_out.at[pl.ds(0, ND - 1)], sc_send)
-    out_copy.wait()
+    own_score.wait()
+    place_copy.wait()
+    bytes_wait(got_hbm.at[pl.ds(0, ND - 1)], sc_recv)
 
 
 def shards(activations, out_grads, proj_in, proj_out, validation, doc_lengths, owner_rows):
@@ -394,11 +385,14 @@
     width_out = out_grads.shape[1]
     dma = pltpu.SemaphoreType.DMA
     any_spec = pl.BlockSpec(memory_space=pl.ANY)
-    return pl.pallas_call(
+    got, place = pl.pallas_call(
         kernel,
-        out_shape=jax.ShapeDtypeStruct((ND, 128), BF16),
+        out_shape=(
+            jax.ShapeDtypeStruct((ND, 1, 128), BF16),
+            jax.ShapeDtypeStruct((ND, ND), BF16),
+        ),
         in_specs=[any_spec] * 7,
-        out_specs=any_spec,
+        out_specs=(any_spec, any_spec),
         scratch_shapes=[
             pltpu.VMEM((tokens, width_in), BF16),
             pltpu.VMEM((tokens, width_out), BF16),
@@ -414,15 +408,14 @@
             pltpu.VMEM((3, ND, 128), F32),
             pltpu.VMEM((ND, 1, 128), F32),
             pltpu.VMEM((ND, 1, 128), F32),
-            pltpu.VMEM((ND, 1, 128), F32),
-            pltpu.VMEM((ND, 1, 128), F32),
+            pltpu.VMEM((ND, 1, 128), BF16),
             pltpu.VMEM((32, 2 * PAIR), F32),
             pltpu.VMEM((32 * ND, 2 * PAIR), BF16),
             pltpu.VMEM((32 * ND, 128), F32),
-            pltpu.VMEM((ND, 128), BF16),
+            pltpu.VMEM((ND, ND), BF16),
             dma((NCH,)),
             dma((NCH,)),
-            dma((7,)),
+            dma((8,)),
             dma((5,)),
             dma((5,)),
             dma((NCH,)),
@@ -437,6 +430,8 @@
         compiler_params=pltpu.CompilerParams(collective_id=0, has_side_effects=True),
         name="sketch_scores",
     )(activations, out_grads, proj_in.T, proj_out.T, validation, doc_lengths, owner_rows)
+    placed = jnp.dot(place, got.reshape(ND, 128), preferred_element_type=F32)
+    return placed.astype(BF16)
 
 
 def solution(mesh):

time: 31 us -> 30 us (0.968)
  matrix products: 0 us -> 1.46 us
  local copies, waits for them, and re-layouts: 1.3 us -> 0 us
  Pallas kernels: 29.5 us -> 28.4 us
    dot_general x0 -> x1, matrix products: none -> 1.46 us  [shards(): placed = jnp.dot(place, got.reshape(ND, 128), preferred_element_type=F32)]
    unnamed x1 -> x0, local copies, waits for them, and re-layouts: 1.3 us -> none
    pallas_call x1, Pallas kernels: 29.5 us -> 28.4 us  [shards(): pl.pallas_call(kernel, out_shape=(jax.ShapeDtypeStruct((ND, 1, 128), BF16...]
where the time goes in v4:
time: 30 us; the launch traced here: 29.8 us
  Pallas kernels  28.4 us (95%)
  matrix products  1.46 us (5%)
    pallas_call x1, Pallas kernels, shards(): pl.pallas_call(kernel, out_shape=(jax.ShapeDtypeStruct((ND, 1, 128), BF16...  28.4 us
    dot_general x1, matrix products, shards(): placed = jnp.dot(place, got.reshape(ND, 128), preferred_element_type=F32)  1.46 us

profile of v4, /device:TPU:1, one launch (start us, length us, event | category | flops | bytes accessed | tf_op | source)
XLA Modules:
  0.0 29.8 jit_solution(5199109387058371516)
XLA Ops:
  0.0 28.4 %sketch_scores.1 = (bf16[32,1,128]{2,1,0:T(2,128)(2,1)}, bf16[32,32]{1,0:T(8,128)(2,1)}) custom-call(bf16[1024,7168]{1,0:T(8,128)(2,1)} %act_hbm.1, bf16[1024,2048]{1,0:T(8,128)(2,1)} %grad_hbm.1, bf16[64,7168]{1,0:T(8,128)(2,1)} %bitcast.6, bf16[64,2048]{1,0:T(8,128)(2,1)} %bitcast.7, bf16[128,128]{1,0:T(8,128)(2,1)} %val_hbm.1, s32[1,32]{1,0:T(1,128)} %len_hbm.1, ...), custom_call_target="tpu_custom_call" | custom-call | tf_op jit(solution)/shard_map/sketch_scores/pallas_call | solution.py:388
  28.4 1.5 %convolution_convert_fusion = bf16[32,128]{1,0:T(8,128)(2,1)} fusion(bf16[32,32]{1,0:T(8,128)(2,1)} %get-tuple-element.7, bf16[32,1,128]{2,1,0:T(2,128)(2,1)} %get-tuple-element.8), kind=kOutput, calls=%fused_computation | convolution fusion | flops 266240 | bytes 18432 | tf_op jit(solution)/shard_map/dot_general | solution.py:433

commit v5 on v4

--- a/solution.py
+++ b/solution.py
@@ -22,6 +22,7 @@
 NT = 4
 ND = 32
 SUB = CH // NT
+HALF = CH // 2
 AHEAD = 3
 
 
@@ -118,13 +119,15 @@
         lab_out[i] = slots_wide[i : i + 1, :]
     s_ref[...] = jnp.zeros_like(s_ref)
 
-    def multiply(c):
-        rows = pl.ds(pl.multiple_of(c * CH, CH), CH)
+    def arrive(c):
         act_copy(c).wait()
         grad_copy(c).wait()
+
+    def multiply(c, first=0, count=CH):
+        rows = pl.ds(pl.multiple_of(c * CH + first, count), count)
         left = lax.dot_general(act_v[rows, :], pin_v[...], NT_DIMS, preferred_element_type=F32)
         right = lax.dot_general(grad_v[rows, :], pout_v[...], NT_DIMS, preferred_element_type=F32)
-        part[c] = jnp.concatenate([left, right], axis=1).astype(BF16)
+        part[c, first : first + count, :] = jnp.concatenate([left, right], axis=1).astype(BF16)
 
     def scatter_copy(c, d):
         peer = lax.rem(t + d, NT)
@@ -137,11 +140,11 @@
             device_id_type=MESH,
         )
 
-    def direct_copy(c, d):
+    def direct_copy(c, d, half):
         peer = lax.rem(t + d, NT)
         return pltpu.make_async_remote_copy(
-            src_ref=part.at[c],
-            dst_ref=dbuf.at[c - NRS, d - 1],
+            src_ref=part.at[c, pl.ds(half, HALF)],
+            dst_ref=dbuf.at[c - NRS, d - 1, pl.ds(half, HALF)],
             send_sem=rs_send.at[c],
             recv_sem=rs_recv.at[c],
             device_id=(r, peer),
@@ -181,6 +184,7 @@
         def _():
             ahead(c)
 
+        arrive(c)
         multiply(c)
         return carry
 
@@ -241,17 +245,11 @@
 
     def step(c, carry):
         ahead(c)
+        arrive(c)
         multiply(c)
 
-        @pl.when(c < NRS)
-        def _():
-            for d in (2, 1, 3):
-                scatter_copy(c, d).start()
-
-        @pl.when(c >= NRS)
-        def _():
-            for d in (2, 1, 3):
-                direct_copy(c, d).start()
+        for d in (2, 1, 3):
+            scatter_copy(c, d).start()
 
         @pl.when(c >= LAG)
         def _():
@@ -263,7 +261,14 @@
 
         return carry
 
-    lax.fori_loop(EARLY, NCH, step, 0)
+    lax.fori_loop(EARLY, NRS, step, 0)
+
+    arrive(NRS)
+    for half in (0, HALF):
+        multiply(NRS, half, HALF)
+        for d in (2, 1, 3):
+            direct_copy(NRS, d, half).start()
+    reduce(NRS - LAG)
     for c in range(NCH - LAG, NRS):
         reduce(c)
 

time: 30 us -> 30 us (level)
  no operation moved by 1% of the time
where the time goes in v5:
time: 30 us; the launch traced here: 29.8 us
  Pallas kernels  28.3 us (94%)
  matrix products  1.46 us (5%)
    pallas_call x1, Pallas kernels, shards(): pl.pallas_call(kernel, out_shape=(jax.ShapeDtypeStruct((ND, 1, 128), BF16...  28.3 us
    dot_general x1, matrix products, shards(): placed = jnp.dot(place, got.reshape(ND, 128), preferred_element_type=F32)  1.46 us

profile of v5, /device:TPU:1, one launch (start us, length us, event | category | flops | bytes accessed | tf_op | source)
XLA Modules:
  0.0 29.8 jit_solution(2311102006932202793)
XLA Ops:
  0.0 28.3 %sketch_scores.1 = (bf16[32,1,128]{2,1,0:T(2,128)(2,1)}, bf16[32,32]{1,0:T(8,128)(2,1)}) custom-call(bf16[1024,7168]{1,0:T(8,128)(2,1)} %act_hbm.1, bf16[1024,2048]{1,0:T(8,128)(2,1)} %grad_hbm.1, bf16[64,7168]{1,0:T(8,128)(2,1)} %bitcast.6, bf16[64,2048]{1,0:T(8,128)(2,1)} %bitcast.7, bf16[128,128]{1,0:T(8,128)(2,1)} %val_hbm.1, s32[1,32]{1,0:T(1,128)} %len_hbm.1, ...), custom_call_target="tpu_custom_call" | custom-call | tf_op jit(solution)/shard_map/sketch_scores/pallas_call | solution.py:393
  28.3 1.5 %convolution_convert_fusion = bf16[32,128]{1,0:T(8,128)(2,1)} fusion(bf16[32,32]{1,0:T(8,128)(2,1)} %get-tuple-element.7, bf16[32,1,128]{2,1,0:T(2,128)(2,1)} %get-tuple-element.8), kind=kOutput, calls=%fused_computation | convolution fusion | flops 266240 | bytes 18432 | tf_op jit(solution)/shard_map/dot_general | solution.py:438
